TPU v7x, 256 devices: a whole 4x4x8 slice. The times are simulated.
256 devices in a mesh: dp: 16 (over y, x), expert: 16 (over z, core).
Axes of the slice: x: 4, y: 4, z: 8, core: 2. Of those that a mesh axis runs over, the one named last changes fastest.
Arguments:
- tokens: bfloat16 [4096, 4096], P('dp', 'expert'), may hold values from -6 to 6
- routing: int32 [4096, 2], P('dp'), may hold values from 0 to 15, all different within a row; in each aligned block of 256 rows (0 to 255, 256 to 511, ...) at most 48 rows name the same one
- gate_weight: bfloat16 [4096, 16], P('expert'), may hold values from -0.09375 to 0.09375
- expert_in: bfloat16 [16, 4096, 8192], P('dp', None, 'expert'), may hold values from -0.09375 to 0.09375
- expert_out: bfloat16 [16, 8192, 4096], P('dp', 'expert'), may hold values from -0.75 to 0.75
Outputs:
- mixed: bfloat16 [4096, 4096], P('dp', 'expert')
Inputs may be any that keep to these rules, and one draw needn't show every extreme that they name: `routing`: each row names two different experts. Within the 256 rows of one group, no expert is named by more than 48 rows, a bound that some block reaches.
All inputs are finite; a program needn't handle non-finite values.
Results may differ from a plain program's by a relative error of at most 0.02.
Values may be sent and summed in bfloat16 or wider, within the bound.
A program may use at most 64 MiB of HBM per device.

v0:
```python
import jax
import jax.numpy as jnp
from jax import lax
from jax.sharding import Mesh
from jax.sharding import PartitionSpec as P

EXPERT = ("expert_0", "expert_1")


def over_axes(value, axes):
    for axis in axes:
        value = lax.psum(value, axis)
    return value


def softmax_rows(logits):
    raised = jnp.exp(logits)
    return raised / jnp.sum(raised, axis=-1, keepdims=True)


def pick_chosen(softmax_all, picks):
    experts = softmax_all.shape[1]
    labels = lax.broadcasted_iota(jnp.int32, (picks.shape[0], 2, experts), 2)
    selected = labels == picks[:, :, None]
    return jnp.sum(jnp.where(selected, softmax_all[:, None, :], 0.0), axis=-1).astype(jnp.bfloat16)


def expert_rows(block_rows, weight_in, weight_out):
    sources = block_rows.shape[0]
    slots_here = block_rows.shape[1]
    width_local = block_rows.shape[2]
    flat_rows = block_rows.reshape(sources * slots_here, width_local)
    pre_act = jnp.dot(
        lax.all_gather(flat_rows, EXPERT, axis=1, tiled=True),
        weight_in,
        preferred_element_type=jnp.float32,
    )
    hidden = jax.nn.gelu(pre_act, approximate=True).astype(jnp.bfloat16)
    partial_out = jnp.dot(hidden, weight_out, preferred_element_type=jnp.float32)
    summed = lax.psum_scatter(
        partial_out.astype(jnp.bfloat16), EXPERT, scatter_dimension=1, tiled=True
    )
    return summed.reshape(sources, slots_here, width_local)


def shards(tokens, routing, gate_weight, expert_in, expert_out):
    group_size = tokens.shape[0]
    width_local = tokens.shape[1]
    experts = gate_weight.shape[1]
    dp_count = lax.axis_size("dp")
    capacity = 3 * group_size // dp_count
    weight_in = expert_in[0]
    weight_out = expert_out[0]
    partial_logits = jnp.dot(tokens, gate_weight, preferred_element_type=jnp.float32)
    logits = over_axes(partial_logits, EXPERT)
    chosen = pick_chosen(softmax_rows(logits), routing)
    order = jnp.concatenate([routing[:, 0], routing[:, 1]], axis=0)
    labels = lax.broadcasted_iota(jnp.int32, (2 * group_size, experts), 1)
    onehot = (labels == order[:, None]).astype(jnp.int32)
    before = jnp.cumsum(onehot, axis=0) - onehot
    slot_flat = jnp.sum(before * onehot, axis=1)
    slot_index = jnp.stack([slot_flat[:group_size], slot_flat[group_size:]], axis=1)
    target = routing * capacity + slot_index
    columns = lax.broadcasted_iota(jnp.int32, (group_size, experts * capacity), 1)
    first_hit = columns == target[:, 0:1]
    second_hit = columns == target[:, 1:2]
    assign = jnp.logical_or(first_hit, second_hit).astype(jnp.bfloat16)
    outgoing = jnp.einsum("gs,gd->sd", assign, tokens, preferred_element_type=jnp.float32)
    outgoing = outgoing.astype(jnp.bfloat16).reshape(experts, capacity, width_local)
    incoming = lax.all_to_all(outgoing, "dp", split_axis=0, concat_axis=0, tiled=True)
    processed = expert_rows(incoming, weight_in, weight_out)
    returned_rows = lax.all_to_all(processed, "dp", split_axis=0, concat_axis=0, tiled=True)
    zero_weight = jnp.zeros((), jnp.bfloat16)
    combine = jnp.where(first_hit, chosen[:, 0:1], zero_weight) + jnp.where(
        second_hit, chosen[:, 1:2], zero_weight
    )
    mixed = jnp.dot(
        combine,
        returned_rows.reshape(experts * capacity, width_local),
        preferred_element_type=jnp.float32,
    )
    return mixed.astype(jnp.bfloat16)


def solution(mesh):
    torus = Mesh(mesh.devices.reshape(mesh.shape["dp"], 8, 2), ("dp", "expert_0", "expert_1"))
    placed = (
        P("dp", EXPERT),
        P("dp", None),
        P(EXPERT, None),
        P("dp", None, EXPERT),
        P("dp", EXPERT, None),
    )
    return jax.shard_map(
        shards, mesh=torus, in_specs=placed, out_specs=P("dp", EXPERT), check_vma=False
    )
```

profile of v0, /device:TPU:2, one launch (start us, length us, event | category | flops | bytes accessed | tf_op | source)
XLA Modules:
  0.0 186.2 jit_solution(17316833488895113456)
XLA Ops:
  6.5 0.0 copy-start
  6.5 0.0 all-gather.2.cloned.1.call-start
  6.5 0.8 fusion.44
  7.3 1.2 reduce-window.6
  8.5 0.2 slice_reduce_fusion
  8.7 0.1 fusion.35
  8.9 0.7 add_add_fusion
  9.6 0.0 copy-done
  9.6 0.6 convolution_convert_fusion.1
  10.2 16.1 %all_to_all.10 = bf16[16,48,256]{2,1,0:T(8,128)(2,1)} all-to-all(bf16[16,48,256]{2,1,0:T(8,128)(2,1)S(1)} %bitcast.49), channel_id=1, replica_groups=mesh['dp'=16,'expert_0'=8,'expert_1'=2] {'dp'}, dimensions={0} | all-to-all | bytes 786432 | tf_op jit(solution)/shard_map/all_to_all | solution.py:70
  26.3 0.0 all-gather.2.cloned.1.call-update
  26.3 0.0 reduce-scatter.2.cloned.1.call-start
  26.3 57.0 %all-gather.2.cloned.1.call-done = bf16[768,4096]{1,0:T(8,128)(2,1)} async-done(((bf16[768,256]{1,0:T(8,128)(2,1)}), bf16[768,4096]{1,0:T(8,128)(2,1)}) %all-gather.2.cloned.1.call-update) | async-done | bytes 6291472 | tf_op jit(solution)/shard_map/all_gather | solution.py:34
  83.3 13.2 %convolution_convert_fusion = bf16[768,4096]{1,0:T(8,128)(2,1)} fusion(bf16[1,512,4096]{2,1,0:T(8,128)(2,1)} %param.9, bf16[768,4096]{1,0:T(8,128)(2,1)} %all-gather.2.cloned.1.call-done, bf16[1,4096,512]{2,1,0:T(8,128)(2,1)} %param.8), kind=kOutput, calls=%fused_computation | convolution fusion | flops 6449135616 | bytes 20971520 | tf_op jit(solution)/shard_map/dot_general | solution.py:39
  96.5 0.0 copy-start.2
  96.5 0.0 copy-start.1
  96.5 0.0 reduce-scatter.2.cloned.1.call-update
  96.5 0.7 copy-done.2
  97.2 0.1 fusion.45
  97.4 29.9 %psum.14 = f32[256,16]{0,1:T(8,128)S(1)} all-reduce(f32[256,16]{0,1:T(8,128)S(1)} %fusion.45), channel_id=1, replica_groups=mesh['dp'=16,'expert_0'=8,'expert_1'=2] {'expert_0'}, use_global_device_ids=true, to_apply=%region_3.4 | all-reduce | flops 4096 | bytes 32768 | tf_op jit(solution)/shard_map/psum | solution.py:12
  127.3 3.3 %psum.15 = f32[256,16]{0,1:T(8,128)S(1)} all-reduce(f32[256,16]{0,1:T(8,128)S(1)} %psum.14), channel_id=1, replica_groups=mesh['dp'=16,'expert_0'=8,'expert_1'=2] {'expert_1'}, use_global_device_ids=true, to_apply=%region_4.5 | all-reduce | flops 4096 | bytes 32768 | tf_op jit(solution)/shard_map/psum | solution.py:12
  130.6 32.4 %reduce-scatter.2.cloned.1.call-done = bf16[768,256]{1,0:T(8,128)(2,1)} async-done(((bf16[768,4096]{1,0:T(8,128)(2,1)}), bf16[768,256]{1,0:T(8,128)(2,1)}) %reduce-scatter.2.cloned.1.call-update) | async-done | bytes 393232 | tf_op jit(solution)/shard_map/reduce_scatter | solution.py:40
  163.0 7.3 %all-to-all-start.1 = ((bf16[16,48,256]{2,1,0:T(8,128)(2,1)}), bf16[16,48,256]{2,1,0:T(8,128)(2,1)S(1)}, u32[]{:S(2)}, u32[]{:S(2)}) async-start(bf16[16,48,256]{2,1,0:T(8,128)(2,1)} %bitcast.47), calls=%async_computation.2 | async-start | bytes 786432 | tf_op jit(solution)/shard_map/all_to_all | solution.py:72
  170.3 0.0 copy-done.1
  170.4 8.0 %all-to-all-done.1 = bf16[16,48,256]{2,1,0:T(8,128)(2,1)S(1)} async-done(((bf16[16,48,256]{2,1,0:T(8,128)(2,1)}), bf16[16,48,256]{2,1,0:T(8,128)(2,1)S(1)}, u32[]{:S(2)}, u32[]{:S(2)}) %all-to-all-start.1) | async-done | bytes 393248 | tf_op jit(solution)/shard_map/all_to_all | solution.py:72
  178.4 1.0 convolution_convert_fusion.2
  (11 shorter events, 0.2 us)
Async XLA Ops:
  6.5 3.0 %copy-start = (bf16[256,256]{1,0:T(8,128)(2,1)S(1)}, bf16[256,256]{1,0:T(8,128)(2,1)}, u32[]{:S(2)}) copy-start(bf16[256,256]{1,0:T(8,128)(2,1)} %param.5) | copy-start | bytes 393220
  6.5 76.8 %all-gather.2.cloned.1.call-start = ((), (), s32[]{:S(2)}) async-start(), calls=%async_computation.3 | async-start | bytes 6684672 | tf_op jit(solution)/shard_map/all_gather | solution.py:34
  26.3 136.8 %reduce-scatter.2.cloned.1.call-start = ((), (), s32[]{:S(2)}) async-start(), calls=%async_computation.4 | async-start | bytes 6684672 | tf_op jit(solution)/shard_map/reduce_scatter | solution.py:40
  96.5 0.7 copy-start.2
  96.5 73.8 %copy-start.1 = (s32[256,2]{0,1:T(2,128)S(1)}, s32[256,2]{0,1:T(2,128)}, u32[]{:S(2)}) copy-start(s32[256,2]{0,1:T(2,128)} %param.6) | copy-start | bytes 6148
  163.0 15.3 %all-to-all-start.1 = ((bf16[16,48,256]{2,1,0:T(8,128)(2,1)}), bf16[16,48,256]{2,1,0:T(8,128)(2,1)S(1)}, u32[]{:S(2)}, u32[]{:S(2)}) async-start(bf16[16,48,256]{2,1,0:T(8,128)(2,1)} %bitcast.47), calls=%async_computation.2 | async-start | bytes 786432 | tf_op jit(solution)/shard_map/all_to_all | solution.py:72
Sparse Core Ops, SparseCore 0:
  26.4 56.8 all-gather.1
  96.7 66.3 reduce-scatter.1
where the time goes:
time: 187 us; the launch traced here: 186 us
  waiting for transfers between devices  97.4 us (52%)
  blocking collectives  49.3 us (26%)
  matrix products  15 us (8%)
  between operations  13.5 us (7%)
  starting transfers between devices  7.33 us (4%)
  other arithmetic  2.06 us (1%)
    all_gather x1, waiting for transfers between devices, expert_rows(): lax.all_gather(flat_rows, EXPERT, axis=1, tiled=True)  57 us
    psum x2, blocking collectives, over_axes(): value = lax.psum(value, axis)  33.2 us
    reduce_scatter x1, waiting for transfers between devices, expert_rows(): lax.psum_scatter(partial_out.astype(jnp.bfloat16), EXPERT, scatter_dimens...  32.4 us
    all_to_all x1, blocking collectives, shards(): lax.all_to_all(outgoing, 'dp', split_axis=0, concat_axis=0, tiled=True)  16.1 us
    dot_general x1, matrix products, expert_rows(): jnp.dot(hidden, weight_out, preferred_element_type=jnp.float32)  13.2 us
    all_to_all x1, waiting for transfers between devices, shards(): lax.all_to_all(processed, 'dp', split_axis=0, concat_axis=0, tiled=True)  7.96 us
    all_to_all x1, starting transfers between devices, shards(): lax.all_to_all(processed, 'dp', split_axis=0, concat_axis=0, tiled=True)  7.29 us
  transfers between devices with their start and end apart: 3, of which 3 were waited for; matrix products, arithmetic and copies ran while one was open for 0% of the time, Pallas kernels for 0%

commit v1 on v0

--- a/solution.py
+++ b/solution.py
@@ -5,6 +5,13 @@
 from jax.sharding import PartitionSpec as P
 
 EXPERT = ("expert_0", "expert_1")
+
+
+def all_by_exchange(shard, name, d):
+    count = lax.axis_size(name)
+    blocks = jnp.stack([shard for _ in range(count)])
+    blocks = lax.all_to_all(blocks, name, split_axis=0, concat_axis=0)
+    return jnp.concatenate(blocks, axis=d)
 
 
 def over_axes(value, axes):
@@ -31,9 +38,7 @@
     width_local = block_rows.shape[2]
     flat_rows = block_rows.reshape(sources * slots_here, width_local)
     pre_act = jnp.dot(
-        lax.all_gather(flat_rows, EXPERT, axis=1, tiled=True),
-        weight_in,
-        preferred_element_type=jnp.float32,
+        all_by_exchange(flat_rows, EXPERT, 1), weight_in, preferred_element_type=jnp.float32
     )
     hidden = jax.nn.gelu(pre_act, approximate=True).astype(jnp.bfloat16)
     partial_out = jnp.dot(hidden, weight_out, preferred_element_type=jnp.float32)

time: 187 us -> 275 us (1.47)
  blocking collectives: 49.3 us -> 195 us
  waiting for transfers between devices: 97.4 us -> 39.2 us
    all_to_all x0 -> x1, blocking collectives: none -> 148 us  [all_by_exchange(): blocks = lax.all_to_all(blocks, name, split_axis=0, concat_axis=0)]
    all_gather x1 -> x0, waiting for transfers between devices: 57 us -> none  [expert_rows(): lax.all_gather(flat_rows, EXPERT, axis=1, tiled=True)]
  transfers between devices with their start and end apart: 3 -> 2, of which waited for: 3 -> 2; matrix products, arithmetic and copies ran while one was open for 0% -> 0% of each run, Pallas kernels for 0% -> 0%
where the time goes in v1:
time: 275 us
  blocking collectives  195 us (71%)
  waiting for transfers between devices  39.2 us (14%)
  matrix products  15.1 us (5%)
  between operations  13.5 us (5%)
  starting transfers between devices  7.5 us (3%)
    all_to_all x1, blocking collectives, all_by_exchange(): blocks = lax.all_to_all(blocks, name, split_axis=0, concat_axis=0)  148 us
    reduce_scatter x1, waiting for transfers between devices, expert_rows(): lax.psum_scatter(partial_out.astype(jnp.bfloat16), EXPERT, scatter_dimens...  31.2 us
    psum x2, blocking collectives, over_axes(): value = lax.psum(value, axis)  31.1 us
    all_to_all x1, blocking collectives, shards(): lax.all_to_all(outgoing, 'dp', split_axis=0, concat_axis=0, tiled=True)  16 us
    dot_general x1, matrix products, expert_rows(): jnp.dot(hidden, weight_out, preferred_element_type=jnp.float32)  13.3 us
    all_to_all x1, waiting for transfers between devices, shards(): lax.all_to_all(processed, 'dp', split_axis=0, concat_axis=0, tiled=True)  7.96 us
    all_to_all x1, starting transfers between devices, shards(): lax.all_to_all(processed, 'dp', split_axis=0, concat_axis=0, tiled=True)  7.5 us
  transfers between devices with their start and end apart: 2, of which 2 were waited for; matrix products, arithmetic and copies ran while one was open for 0% of the time, Pallas kernels for 0%

profile of v1, /device:TPU:2, one launch (start us, length us, event | category | flops | bytes accessed | tf_op | source)
XLA Modules:
  0.0 274.8 jit_solution(15729630038480206925)
XLA Ops:
  6.5 0.0 copy-start
  6.5 0.0 reduce-scatter.2.cloned.1.call-start
  6.5 0.8 fusion.40
  7.3 1.2 reduce-window.6
  8.5 0.2 slice_reduce_fusion
  8.7 0.1 fusion.31
  8.9 0.7 add_add_fusion
  9.6 0.0 copy-done
  9.6 0.6 convolution_convert_fusion.1
  10.2 16.0 %all_to_all.15 = bf16[16,48,256]{2,1,0:T(8,128)(2,1)S(1)} all-to-all(bf16[16,48,256]{2,1,0:T(8,128)(2,1)S(1)} %bitcast.53), channel_id=1, replica_groups=mesh['dp'=16,'expert_0'=8,'expert_1'=2] {'dp'}, dimensions={0} | all-to-all | bytes 786432 | tf_op jit(solution)/shard_map/all_to_all | solution.py:75
  26.2 0.2 copy.13
  26.3 0.6 stack.15
  26.9 148.0 %all_to_all.16 = bf16[16,768,256]{1,2,0:T(8,128)(2,1)} all-to-all(bf16[16,768,256]{1,2,0:T(8,128)(2,1)S(1)} %stack.15), channel_id=1, replica_groups=mesh['dp'=16,'expert_0'=8,'expert_1'=2] {'expert_0','expert_1'}, dimensions={0} | all-to-all | bytes 12582912 | tf_op jit(solution)/shard_map/all_to_all | solution.py:13
  175.0 13.3 %convolution_convert_fusion = bf16[768,4096]{1,0:T(8,128)(2,1)} fusion(bf16[1,512,4096]{2,1,0:T(8,128)(2,1)} %param.9, bf16[768,4096]{0,1:T(8,128)(2,1)} %bitcast.49, bf16[1,4096,512]{2,1,0:T(8,128)(2,1)} %param.8), kind=kOutput, calls=%fused_computation | convolution fusion | flops 6449135616 | bytes 20971520 | tf_op jit(solution)/shard_map/dot_general | solution.py:44
  188.3 0.0 copy-start.2
  188.3 0.0 copy-start.1
  188.3 0.0 reduce-scatter.2.cloned.1.call-update
  188.3 0.7 copy-done.2
  189.0 0.1 fusion.41
  189.1 27.7 %psum.14 = f32[256,16]{0,1:T(8,128)S(1)} all-reduce(f32[256,16]{0,1:T(8,128)S(1)} %fusion.41), channel_id=1, replica_groups=mesh['dp'=16,'expert_0'=8,'expert_1'=2] {'expert_0'}, use_global_device_ids=true, to_apply=%region_3.4 | all-reduce | flops 4096 | bytes 32768 | tf_op jit(solution)/shard_map/psum | solution.py:19
  216.9 3.3 %psum.15 = f32[256,16]{0,1:T(8,128)S(1)} all-reduce(f32[256,16]{0,1:T(8,128)S(1)} %psum.14), channel_id=1, replica_groups=mesh['dp'=16,'expert_0'=8,'expert_1'=2] {'expert_1'}, use_global_device_ids=true, to_apply=%region_4.5 | all-reduce | flops 4096 | bytes 32768 | tf_op jit(solution)/shard_map/psum | solution.py:19
  220.2 31.2 %reduce-scatter.2.cloned.1.call-done = bf16[768,256]{1,0:T(8,128)(2,1)} async-done(((bf16[768,4096]{1,0:T(8,128)(2,1)}), bf16[768,256]{1,0:T(8,128)(2,1)}) %reduce-scatter.2.cloned.1.call-update) | async-done | bytes 393232 | tf_op jit(solution)/shard_map/reduce_scatter | solution.py:45
  251.4 7.5 %all-to-all-start.2 = ((bf16[16,48,256]{2,1,0:T(8,128)(2,1)}), bf16[16,48,256]{2,1,0:T(8,128)(2,1)S(1)}, u32[]{:S(2)}, u32[]{:S(2)}) async-start(bf16[16,48,256]{2,1,0:T(8,128)(2,1)} %bitcast.51), calls=%async_computation.3 | async-start | bytes 786432 | tf_op jit(solution)/shard_map/all_to_all | solution.py:77
  258.9 0.0 copy-done.1
  259.0 8.0 %all-to-all-done.2 = bf16[16,48,256]{2,1,0:T(8,128)(2,1)S(1)} async-done(((bf16[16,48,256]{2,1,0:T(8,128)(2,1)}), bf16[16,48,256]{2,1,0:T(8,128)(2,1)S(1)}, u32[]{:S(2)}, u32[]{:S(2)}) %all-to-all-start.2) | async-done | bytes 393248 | tf_op jit(solution)/shard_map/all_to_all | solution.py:77
  267.0 1.0 convolution_convert_fusion.2
  (11 shorter events, 0.2 us)
Async XLA Ops:
  6.5 3.0 %copy-start = (bf16[256,256]{1,0:T(8,128)(2,1)S(1)}, bf16[256,256]{1,0:T(8,128)(2,1)}, u32[]{:S(2)}) copy-start(bf16[256,256]{1,0:T(8,128)(2,1)} %param.5) | copy-start | bytes 393220
  6.5 244.9 %reduce-scatter.2.cloned.1.call-start = ((), (), s32[]{:S(2)}) async-start(), calls=%async_computation.4 | async-start | bytes 6684672 | tf_op jit(solution)/shard_map/reduce_scatter | solution.py:45
  188.3 0.7 copy-start.2
  188.3 70.6 %copy-start.1 = (s32[256,2]{0,1:T(2,128)S(1)}, s32[256,2]{0,1:T(2,128)}, u32[]{:S(2)}) copy-start(s32[256,2]{0,1:T(2,128)} %param.6) | copy-start | bytes 6148
  251.4 15.5 %all-to-all-start.2 = ((bf16[16,48,256]{2,1,0:T(8,128)(2,1)}), bf16[16,48,256]{2,1,0:T(8,128)(2,1)S(1)}, u32[]{:S(2)}, u32[]{:S(2)}) async-start(bf16[16,48,256]{2,1,0:T(8,128)(2,1)} %bitcast.51), calls=%async_computation.3 | async-start | bytes 786432 | tf_op jit(solution)/shard_map/all_to_all | solution.py:77
Sparse Core Ops, SparseCore 0:
  188.4 62.9 reduce-scatter.1
